TPU v7x, 256 devices: a whole 4x4x8 slice. The times are simulated.
256 devices in a mesh: dp: 8 (over x, core), expert: 32 (over z, y).
Axes of the slice: x: 4, y: 4, z: 8, core: 2. Of those that a mesh axis runs over, the one named last changes fastest.
Arguments:
- tokens: bfloat16 [2048, 6144], P('dp', 'expert'), may hold values from -6 to 6
- cotangent: bfloat16 [2048, 6144], P('dp', 'expert'), may hold values from -6 to 6
- expert_choice: int32 [2048, 2], P('dp'), may hold values from 0 to 7, all different within a row; in each aligned block of 256 rows (0 to 255, 256 to 511, ...) at most 80 rows name the same one
- gate_values: bfloat16 [2048, 2], P('dp'), may hold values from 0.099609375 to 1
- gate_weight: bfloat16 [8, 6144, 8192], P('dp', None, 'expert'), may hold values from -0.078125 to 0.078125
- up_weight: bfloat16 [8, 6144, 8192], P('dp', None, 'expert'), may hold values from -0.078125 to 0.078125
- down_weight: bfloat16 [8, 8192, 6144], P('dp', 'expert'), may hold values from -0.0625 to 0.0625
- shrinker: bfloat16 [8, 32, 6144], P('dp'), may hold values from -0.078125 to 0.078125
- widener: bfloat16 [8, 2, 16, 8192], P('dp', None, None, 'expert'), may hold values from -0.375 to 0.375
- squeezer: bfloat16 [8, 16, 8192], P('dp', None, 'expert'), may hold values from -0.0625 to 0.0625
- spreader: bfloat16 [8, 16, 6144], P('dp'), may hold values from -0.375 to 0.375
Outputs:
- token_grad: bfloat16 [2048, 6144], P('dp', 'expert')
- gate_grad: float32 [2048, 2], P('dp')
- shrinker_grad: float32 [8, 32, 6144], P('dp')
- widener_grad: float32 [8, 2, 16, 8192], P('dp', None, None, 'expert')
- squeezer_grad: float32 [8, 16, 8192], P('dp', None, 'expert')
- spreader_grad: float32 [8, 16, 6144], P('dp')
Inputs may be any that keep to these rules, and one draw needn't show every extreme that they name: `expert_choice`: each row names 2 different experts. Among the 256 tokens of one index of dp no expert is chosen more than 80 times, and some expert is chosen exactly 80 times by the tokens of some or all indices of dp.
All inputs are finite; a program needn't handle non-finite values.
Results may differ from a plain program's by a relative error of at most 0.02.
Values may be sent and summed in bfloat16 or wider, within the bound.
No kernel may reach another device: no remote copies, remote signals or barrier semaphores. Data moves between devices by JAX's collectives and lax.ppermute only.
A program may use at most 128 MiB of HBM per device.

v0:
```python
import jax
import jax.numpy as jnp
from jax import lax
from jax.sharding import PartitionSpec as P

adapter_scale = 2.0


def product(pattern, operand_a, operand_b):
    return jnp.einsum(pattern, operand_a, operand_b, preferred_element_type=jnp.float32)


def silu_pair(gate_pre):
    logistic = jax.nn.sigmoid(gate_pre)
    return (gate_pre * logistic, logistic * (1.0 + gate_pre * (1.0 - logistic)))


def full_rows(gathered, capacity, part_width):
    n_groups = gathered.shape[0]
    n_sources = gathered.shape[1]
    ordered = gathered.reshape(n_groups, n_sources, capacity, part_width).transpose(1, 2, 0, 3)
    return ordered.reshape(n_sources * capacity, n_groups * part_width)


def local(
    tokens,
    cotangent,
    expert_choice,
    gate_values,
    gate_weight,
    up_weight,
    down_weight,
    shrinker,
    widener,
    squeezer,
    spreader,
):
    tok_rows, part_width = tokens.shape
    top_k = expert_choice.shape[1]
    low_rank = spreader.shape[1]
    n_groups = lax.axis_size("expert")
    n_experts = lax.axis_size("dp")
    capacity = tok_rows * top_k * 5 // (4 * n_experts)
    own_rows = n_experts * capacity
    flat_choice = expert_choice.reshape(-1)
    onehot = (flat_choice[:, None] == jnp.arange(n_experts, dtype=jnp.int32)[None, :]).astype(
        jnp.int32
    )
    before = jnp.cumsum(onehot, axis=0) - onehot
    slot_index = jnp.sum(before * onehot, axis=1)
    target = flat_choice * capacity + slot_index
    placing = target[None, :] == jnp.arange(own_rows, dtype=jnp.int32)[:, None]
    stacked = jnp.repeat(jnp.concatenate([tokens, cotangent], axis=1), top_k, axis=0)
    placed = jnp.dot(
        placing.astype(jnp.bfloat16), stacked, preferred_element_type=jnp.float32
    ).astype(jnp.bfloat16)
    send_x = placed[:, :part_width].reshape(n_experts, capacity * part_width)
    send_dy = placed[:, part_width:].reshape(n_experts, capacity * part_width)
    gate_flat = gate_values.reshape(-1).astype(jnp.float32)
    send_gate = (
        jnp.sum(jnp.where(placing, gate_flat[None, :], 0.0), axis=1)
        .astype(jnp.bfloat16)
        .reshape(n_experts, capacity)
    )
    recv_x, recv_dy, recv_gate = (
        lax.all_to_all(send_x, "dp", split_axis=0, concat_axis=0, tiled=True),
        lax.all_to_all(send_dy, "dp", split_axis=0, concat_axis=0, tiled=True),
        lax.all_to_all(send_gate, "dp", split_axis=0, concat_axis=0, tiled=True),
    )
    gate_rows = recv_gate.reshape(-1).astype(jnp.float32)
    gathered_x, gathered_dy = (
        lax.all_gather(recv_x[None], "expert", axis=0, tiled=True),
        lax.all_gather(recv_dy[None], "expert", axis=0, tiled=True),
    )
    rows_dy = full_rows(gathered_dy, capacity, part_width)
    rows_x = full_rows(gathered_x, capacity, part_width)
    shrink_local = shrinker[0]
    widen_local = widener[0]
    squeeze_local = squeezer[0]
    spread_local = spreader[0]
    lowrank_in = product("nd,rd->nr", rows_x, shrink_local).astype(jnp.bfloat16)
    gate_pre = jnp.dot(
        rows_x, gate_weight[0], preferred_element_type=jnp.float32
    ) + adapter_scale * jnp.dot(
        lowrank_in[:, :low_rank], widen_local[0], preferred_element_type=jnp.float32
    )
    up_pre = jnp.dot(
        rows_x, up_weight[0], preferred_element_type=jnp.float32
    ) + adapter_scale * jnp.dot(
        lowrank_in[:, low_rank:], widen_local[1], preferred_element_type=jnp.float32
    )
    silu_gate, silu_slope = silu_pair(gate_pre)
    activation = (silu_gate * up_pre).astype(jnp.bfloat16)
    out_part = product("rf,nf->rn", squeeze_local, activation)
    out_low = lax.psum(out_part.astype(jnp.bfloat16), "expert").astype(jnp.float32)
    back_down = product("nd,fd->nf", rows_dy, down_weight[0])
    back_low = product("rd,nd->rn", spread_local, rows_dy)
    gate_part = jnp.sum(activation.astype(jnp.float32) * back_down, axis=1)
    scaled_low = (back_low * gate_rows[None, :]).astype(jnp.bfloat16)
    act_delta = gate_rows[:, None] * back_down + adapter_scale * product(
        "rn,rf->nf", scaled_low, squeeze_local
    )
    gate_delta = (act_delta * up_pre * silu_slope).astype(jnp.bfloat16)
    up_delta = (act_delta * silu_gate).astype(jnp.bfloat16)
    back_part = jnp.concatenate(
        [
            product("rf,nf->rn", widen_local[0], gate_delta),
            product("rf,nf->rn", widen_local[1], up_delta),
        ],
        axis=0,
    )
    back_sum, gate_sum = (
        lax.psum(back_part.astype(jnp.bfloat16), "expert").astype(jnp.float32),
        lax.psum(gate_part.astype(jnp.bfloat16), "expert").astype(jnp.float32),
    )
    low_out = out_low.astype(jnp.bfloat16)
    gate_dots = gate_sum + adapter_scale * jnp.sum(low_out.astype(jnp.float32) * back_low, axis=0)
    back_in = back_sum.astype(jnp.bfloat16)
    gate_blocks = gate_weight[0].reshape(n_groups, part_width, gate_weight.shape[2])
    up_blocks = up_weight[0].reshape(n_groups, part_width, up_weight.shape[2])
    term = product("nf,kdf->knd", gate_delta, gate_blocks) + product(
        "nf,kdf->knd", up_delta, up_blocks
    )
    token_part = (
        lax.psum_scatter(
            term.reshape(1 * lax.axis_size("expert"), own_rows * part_width).astype(jnp.bfloat16),
            "expert",
            scatter_dimension=0,
            tiled=True,
        )
        .astype(jnp.float32)
        .reshape(own_rows, part_width)
    )
    shrink_cols = lax.dynamic_slice_in_dim(
        shrink_local, lax.axis_index("expert") * part_width, part_width, 1
    )
    token_part = token_part + adapter_scale * product("rn,rd->nd", back_in, shrink_cols)
    token_back, gate_back = (
        lax.all_to_all(
            token_part.reshape(n_experts, capacity * part_width).astype(jnp.bfloat16),
            "dp",
            split_axis=0,
            concat_axis=0,
            tiled=True,
        ).astype(jnp.float32),
        lax.all_to_all(
            gate_dots.reshape(n_experts, capacity).astype(jnp.bfloat16),
            "dp",
            split_axis=0,
            concat_axis=0,
            tiled=True,
        ).astype(jnp.float32),
    )
    picked = jnp.take(token_back.reshape(own_rows, part_width), target, axis=0)
    token_grad = jnp.sum(picked.reshape(tok_rows, top_k, part_width), axis=1).astype(jnp.bfloat16)
    gate_grad = jnp.take(gate_back.reshape(own_rows), target).reshape(tok_rows, top_k)
    shrinker_grad = adapter_scale * product("rn,nd->rd", back_in, rows_x)
    widener_grad = adapter_scale * jnp.stack(
        [
            product("nr,nf->rf", lowrank_in[:, :low_rank], gate_delta),
            product("nr,nf->rf", lowrank_in[:, low_rank:], up_delta),
        ]
    )
    squeezer_grad = adapter_scale * product("rn,nf->rf", scaled_low, activation)
    weighted_low = (out_low * gate_rows[None, :]).astype(jnp.bfloat16)
    spreader_grad = adapter_scale * product("rn,nd->rd", weighted_low, rows_dy)
    return (
        token_grad,
        gate_grad,
        shrinker_grad[None],
        widener_grad[None],
        squeezer_grad[None],
        spreader_grad[None],
    )


def solution(mesh):
    placed = (
        P("dp", "expert"),
        P("dp", "expert"),
        P("dp", None),
        P("dp", None),
        P("dp", None, "expert"),
        P("dp", None, "expert"),
        P("dp", "expert", None),
        P("dp", None, None),
        P("dp", None, None, "expert"),
        P("dp", None, "expert"),
        P("dp", None, None),
    )
    return jax.shard_map(
        local,
        mesh=mesh,
        in_specs=placed,
        out_specs=(
            P("dp", "expert"),
            P("dp", None),
            P("dp", None, None),
            P("dp", None, None, "expert"),
            P("dp", None, "expert"),
            P("dp", None, None),
        ),
        check_vma=False,
    )
```

profile of v0, /device:TPU:1, one launch (start us, length us, event | category | flops | bytes accessed | tf_op | source)
XLA Modules:
  0.0 594.0 jit_solution(10980135344185267276)
XLA Ops:
  11.8 1.9 broadcast_in_dim.57
  13.7 1.9 reshape.230
  18.7 2.1 all_to_all.31
  21.3 3.0 reduce.16
  25.2 12.8 %all_to_all.38 = bf16[8,2,7680]{2,1,0:T(2,128)(2,1)S(1)} all-to-all(bf16[8,2,7680]{2,1,0:T(2,128)(2,1)} %reshape.290), channel_id=1, replica_groups=mesh['dp'=8,'expert'=32] {'dp'}, dimensions={0} | all-to-all | bytes 491520 | tf_op jit(solution)/shard_map/all_to_all | solution.py:67
  39.0 1.8 copy.92
  40.8 1.8 copy.95
  42.7 2.1 all_to_all.32
  44.8 3.0 reduce.17
  48.7 10.7 %all_to_all.39 = bf16[8,2,7680]{2,1,0:T(2,128)(2,1)S(1)} all-to-all(bf16[8,2,7680]{2,1,0:T(2,128)(2,1)} %reshape.288), channel_id=1, replica_groups=mesh['dp'=8,'expert'=32] {'dp'}, dimensions={0} | all-to-all | bytes 491520 | tf_op jit(solution)/shard_map/all_to_all | solution.py:66
  60.2 1.8 copy.97
  62.7 8.1 %all_to_all.40 = bf16[8,1,80]{2,1,0:T(2,128)(2,1)S(1)} all-to-all(bf16[8,1,80]{2,1,0:T(2,128)(2,1)S(1)} %convert_element_type.180), channel_id=1, replica_groups=mesh['dp'=8,'expert'=32] {'dp'}, dimensions={0} | all-to-all | bytes 2560 | tf_op jit(solution)/shard_map/all_to_all | solution.py:68
  70.9 65.3 %all-gather.5.cloned.1.call-done = bf16[256,1,15360]{2,0,1:T(8,128)(2,1)} async-done(((bf16[8,1,15360]{2,0,1:T(8,128)(2,1)}), bf16[256,1,15360]{2,0,1:T(8,128)(2,1)}) %all-gather.5.cloned.1.call-update) | async-done | bytes 7864336 | tf_op jit(solution)/shard_map/all_gather | solution.py:73
  136.2 18.1 %reshape.231 = bf16[32,8,80,192]{3,2,1,0:T(8,128)(2,1)} reshape(bf16[256,1,15360]{2,0,1:T(8,128)(2,1)} %all-gather.5.cloned.1.call-done) | data formatting | bytes 15728640 | tf_op jit(solution)/shard_map/reshape | solution.py:21
  154.3 13.9 %copy.93 = bf16[8,80,32,192]{3,2,1,0:T(8,128)(2,1)} copy(bf16[8,80,32,192]{3,1,0,2:T(8,128)(2,1)} %bitcast.103) | data formatting | bytes 15728640 | tf_op jit(solution)/shard_map/transpose | solution.py:21
  168.2 18.2 %reshape.232 = bf16[640,6144]{1,0:T(8,128)(2,1)} reshape(bf16[8,80,32,192]{3,2,1,0:T(8,128)(2,1)} %copy.93) | data formatting | bytes 15728640 | tf_op jit(solution)/shard_map/reshape | solution.py:22
  186.4 6.0 %convolution_bitcast_fusion = f32[16,640]{1,0:T(8,128)S(1)} fusion(bf16[640,6144]{1,0:T(8,128)(2,1)} %reshape.232, bf16[1,16,6144]{2,1,0:T(8,128)(2,1)S(1)} %copy-done.8), kind=kOutput, calls=%fused_computation.28 | convolution fusion | flops 125829120 | bytes 8101888 | tf_op jit(solution)/shard_map/rd,nd->rn/dot_general | solution.py:10
  192.4 5.4 fusion.7
  197.8 33.9 %all-gather.7.cloned.1.call-done = bf16[256,1,15360]{2,0,1:T(8,128)(2,1)} async-done(((bf16[8,1,15360]{2,0,1:T(8,128)(2,1)}), bf16[256,1,15360]{2,0,1:T(8,128)(2,1)}) %all-gather.7.cloned.1.call-update) | async-done | bytes 7864336 | tf_op jit(solution)/shard_map/all_gather | solution.py:72
  231.7 18.3 %reshape.233 = bf16[32,8,80,192]{3,2,1,0:T(8,128)(2,1)} reshape(bf16[256,1,15360]{2,0,1:T(8,128)(2,1)} %all-gather.7.cloned.1.call-done) | data formatting | bytes 15728640 | tf_op jit(solution)/shard_map/reshape | solution.py:21
  249.9 13.8 %copy.98 = bf16[8,80,32,192]{3,2,1,0:T(8,128)(2,1)} copy(bf16[8,80,32,192]{3,1,0,2:T(8,128)(2,1)} %bitcast.104) | data formatting | bytes 15728640 | tf_op jit(solution)/shard_map/transpose | solution.py:21
  263.8 18.5 %reshape.234 = bf16[640,6144]{1,0:T(8,128)(2,1)} reshape(bf16[8,80,32,192]{3,2,1,0:T(8,128)(2,1)} %copy.98) | data formatting | bytes 15728640 | tf_op jit(solution)/shard_map/reshape | solution.py:22
  282.3 5.8 convolution_convert_fusion
  288.1 2.9 fusion.3
  291.1 2.9 fusion.5
  295.9 6.8 %fusion.25 = f32[640,32,192]{0,2,1:T(8,128)} fusion(bf16[32,192,256]{2,1,0:T(8,128)(2,1)S(1)} %bitcast.102, bf16[640,256]{0,1:T(8,128)(2,1)S(1)} %get-tuple-element.37), kind=kOutput, calls=%fused_computation.53 | convolution fusion | flops 2013265920 | bytes 19202048 | tf_op jit(solution)/shard_map/nf,kdf->knd/dot_general | solution.py:10
  302.7 8.8 %fusion.2 = bf16[32,640,192]{1,2,0:T(8,128)(2,1)} fusion(f32[640,32,192]{0,2,1:T(8,128)} %fusion.25, bf16[32,192,256]{2,1,0:T(8,128)(2,1)S(1)} %bitcast.105, bf16[640,256]{0,1:T(8,128)(2,1)S(1)} %get-tuple-element.38), kind=kOutput, calls=%fused_computation.7 | convolution fusion | flops 2021130240 | bytes 27066368 | tf_op jit(solution)/shard_map/nf,kdf->knd/dot_general | solution.py:10
  311.6 13.7 %copy.101 = bf16[32,640,192]{2,1,0:T(8,128)(2,1)} copy(bf16[32,640,192]{1,2,0:T(8,128)(2,1)} %fusion.2) | data formatting | bytes 15728640 | tf_op jit(solution)/shard_map/convert_element_type | solution.py:126
  325.3 15.6 %convert_element_type.158 = bf16[32,122880]{1,0:T(8,128)(2,1)} reshape(bf16[32,640,192]{2,1,0:T(8,128)(2,1)} %copy.101) | data formatting | bytes 15728640 | tf_op jit(solution)/shard_map/convert_element_type | solution.py:126
  345.9 114.8 %all-reduce.1 = (bf16[32,640]{1,0:T(8,128)(2,1)S(1)}, bf16[16,640]{1,0:T(8,128)(2,1)S(1)}, bf16[640]{0:T(1024)(128)(2,1)S(1)}) all-reduce(bf16[32,640]{1,0:T(8,128)(2,1)S(1)} %pad_maximum_fusion.1, bf16[16,640]{1,0:T(8,128)(2,1)S(1)} %fusion.18, bf16[640]{0:T(1024)(128)(2,1)S(1)} %get-tuple-element.35), channel_id=1, replica_groups=mesh['dp'=8,'expert'=32] {'expert'}, use_global_device_ids=true, to_apply=%region_5.6 | all-reduce | flops 31360 | bytes 125440 | tf_op jit(solution)/shard_map/psum | solution.py:113
  461.4 32.7 %all-to-all-start.4 = ((bf16[8,1,80]{2,1,0:T(2,128)(2,1)}), bf16[8,1,80]{2,1,0:T(2,128)(2,1)S(1)}, u32[]{:S(2)}, u32[]{:S(2)}) async-start(bf16[8,1,80]{2,1,0:T(2,128)(2,1)} %convert_element_type.182), calls=%async_computation.4 | async-start | bytes 8192 | tf_op jit(solution)/shard_map/all_to_all | solution.py:146
  496.4 1.9 fusion.19
  498.3 5.3 fusion.1
  503.5 5.7 fusion
  509.9 2.3 gather_fusion.1
  513.0 30.8 %all-reduce.4.cloned.1.call-done = bf16[32,122880]{1,0:T(8,128)(2,1)} async-done(((bf16[32,122880]{1,0:T(8,128)(2,1)}), bf16[32,122880]{1,0:T(8,128)(2,1)}) %all-reduce.4.cloned.1.call-update) | async-done | bytes 7864336
  543.8 4.4 fusion.22
  548.3 2.0 reshape.240
  550.3 2.1 copy.102
  554.7 2.1 convert_element_type.181
  556.8 3.0 reduce.18
  560.7 5.4 all-to-all-start.3
  569.4 3.0 all-to-all-done.3
  573.3 3.2 convert_reduce_fusion
  576.5 2.2 reshape.241
  578.6 3.3 gather_fusion
  581.9 2.1 gather.13
  584.1 2.4 select_reduce_fusion.1
  (90 shorter events, 32.1 us)
Async XLA Ops:
  7.2 280.9 %copy-start = (bf16[1,6144,256]{2,1,0:T(8,128)(2,1)S(1)}, bf16[1,6144,256]{2,1,0:T(8,128)(2,1)}, u32[]{:S(2)}) copy-start(bf16[1,6144,256]{2,1,0:T(8,128)(2,1)} %param.15) | copy-start | bytes 9437188
  7.2 54.9 %copy-start.12 = (bf16[256,2]{0,1:T(2,128)(2,1)S(1)}, bf16[256,2]{0,1:T(2,128)(2,1)}, u32[]{:S(2)}) copy-start(bf16[256,2]{0,1:T(2,128)(2,1)} %param.14) | copy-start | bytes 3076
  7.2 129.0 %all-gather.5.cloned.1.call-start = ((), (), s32[]{:S(2)}) async-start(), calls=%async_computation.5 | async-start | bytes 8110080 | tf_op jit(solution)/shard_map/all_gather | solution.py:73
  40.8 190.9 %all-gather.7.cloned.1.call-start = ((), (), s32[]{:S(2)}) async-start(), calls=%async_computation.6 | async-start | bytes 8110080 | tf_op jit(solution)/shard_map/all_gather | solution.py:72
  62.1 481.8 %all-reduce.4.cloned.1.call-start = ((), (), s32[]{:S(2)}) async-start(), calls=%async_computation.7 | async-start | bytes 15728640
  168.2 18.2 %copy-start.8 = (bf16[1,16,6144]{2,1,0:T(8,128)(2,1)S(1)}, bf16[1,16,6144]{2,1,0:T(8,128)(2,1)}, u32[]{:S(2)}) copy-start(bf16[1,16,6144]{2,1,0:T(8,128)(2,1)} %param.21) | copy-start | bytes 589828
  186.4 6.0 %copy-start.1 = (bf16[640,6144]{1,0:T(8,128)(2,1)S(1)}, bf16[640,6144]{1,0:T(8,128)(2,1)}, u32[]{:S(2)}) copy-start(bf16[640,6144]{1,0:T(8,128)(2,1)} %reshape.232) | copy-start | bytes 23592964
  282.3 5.8 copy-start.2
  288.1 2.9 copy-start.3
  291.0 3.0 copy-start.10
  291.0 3.3 copy-start.6
  291.0 3.3 copy-start.11
  295.9 6.8 %copy-start.5 = (bf16[640,256]{0,1:T(8,128)(2,1)}, bf16[640,256]{0,1:T(8,128)(2,1)S(1)}, u32[]{:S(2)}) copy-start(bf16[640,256]{0,1:T(8,128)(2,1)S(1)} %get-tuple-element.37) | copy-start | bytes 983044
  295.9 6.8 %copy-start.4 = (bf16[640,256]{0,1:T(8,128)(2,1)}, bf16[640,256]{0,1:T(8,128)(2,1)S(1)}, u32[]{:S(2)}) copy-start(bf16[640,256]{0,1:T(8,128)(2,1)S(1)} %get-tuple-element.38) | copy-start | bytes 983044
  340.8 1.0 copy-start.13
  460.7 48.6 %copy-start.7 = (bf16[32,640]{1,0:T(8,128)(2,1)}, bf16[32,640]{1,0:T(8,128)(2,1)S(1)}, u32[]{:S(2)}) copy-start(bf16[32,640]{1,0:T(8,128)(2,1)S(1)} %get-tuple-element.30) | copy-start | bytes 122884
  461.4 48.5 %all-to-all-start.4 = ((bf16[8,1,80]{2,1,0:T(2,128)(2,1)}), bf16[8,1,80]{2,1,0:T(2,128)(2,1)S(1)}, u32[]{:S(2)}, u32[]{:S(2)}) async-start(bf16[8,1,80]{2,1,0:T(2,128)(2,1)} %convert_element_type.182), calls=%async_computation.4 | async-start | bytes 8192 | tf_op jit(solution)/shard_map/all_to_all | solution.py:146
  560.7 11.7 %all-to-all-start.3 = ((bf16[8,2,7680]{2,1,0:T(2,128)(2,1)}), bf16[8,2,7680]{2,1,0:T(2,128)(2,1)S(1)}, u32[]{:S(2)}, u32[]{:S(2)}) async-start(bf16[8,2,7680]{2,1,0:T(2,128)(2,1)} %reshape.292), calls=%async_computation.3 | async-start | bytes 491520 | tf_op jit(solution)/shard_map/all_to_all | solution.py:139
  573.3 10.8 %copy-start.9 = (pred[256,2]{1,0:T(8,128)(4,1)S(1)}, pred[256,2]{1,0:T(8,128)(4,1)}, u32[]{:S(2)}) copy-start(pred[256,2]{1,0:T(8,128)(4,1)} %get-tuple-element.34) | copy-start | bytes 1540
Sparse Core Ops, SparseCore 0:
  40.9 95.2 all-gather.4
  139.3 92.2 all-gather.6
  341.0 202.8 all-reduce.3
where the time goes:
time: 603 us; the launch traced here: 594 us
  local copies, waits for them, and re-layouts  176 us (29%)
  blocking collectives  146 us (24%)
  waiting for transfers between devices  133 us (22%)
  matrix products  62 us (10%)
  starting transfers between devices  38.3 us (6%)
  other arithmetic  24 us (4%)
  between operations  14.3 us (2%)
    psum x1, blocking collectives, local(): lax.psum(back_part.astype(jnp.bfloat16), 'expert').astype(jnp.float32)  115 us
    all_gather x1, waiting for transfers between devices, local(): lax.all_gather(recv_dy[None], 'expert', axis=0, tiled=True)  65.3 us
    dot_general x15, matrix products, product(): jnp.einsum(pattern, operand_a, operand_b, preferred_element_type=jnp.floa...  53.1 us
    reshape x2, local copies, waits for them, and re-layouts, full_rows(): return ordered.reshape(n_sources * capacity, n_groups * part_width)  36.7 us
    reshape x2, local copies, waits for them, and re-layouts, full_rows(): gathered.reshape(n_groups, n_sources, capacity, part_width)  36.4 us
    all_gather x1, waiting for transfers between devices, local(): lax.all_gather(recv_x[None], 'expert', axis=0, tiled=True)  33.9 us
    all_to_all x1, starting transfers between devices, local(): lax.all_to_all(gate_dots.reshape(n_experts, capacity).astype(jnp.bfloat16...  32.7 us
    unnamed x4, waiting for transfers between devices  30.9 us
  transfers between devices with their start and end apart: 5, of which 4 were waited for; matrix products, arithmetic and copies ran while one was open for 17% of the time, Pallas kernels for 0%

commit v1 on v0

--- a/solution.py
+++ b/solution.py
@@ -4,6 +4,11 @@
 from jax.sharding import PartitionSpec as P
 
 adapter_scale = 2.0
+
+
+def turn_halves(array_here):
+    response = lax.all_to_all(jnp.stack(lax.axis_size("expert") * [array_here], 0), "expert", 0, 0)
+    return jnp.concatenate(response, axis=0)
 
 
 def product(pattern, operand_a, operand_b):
@@ -70,7 +75,7 @@
     gate_rows = recv_gate.reshape(-1).astype(jnp.float32)
     gathered_x, gathered_dy = (
         lax.all_gather(recv_x[None], "expert", axis=0, tiled=True),
-        lax.all_gather(recv_dy[None], "expert", axis=0, tiled=True),
+        turn_halves(recv_dy[None]),
     )
     rows_dy = full_rows(gathered_dy, capacity, part_width)
     rows_x = full_rows(gathered_x, capacity, part_width)

time: 603 us -> 729 us (1.21)
  waiting for transfers between devices: 133 us -> 251 us
  blocking collectives: 146 us -> 118 us
  starting transfers between devices: 38.3 us -> 66.3 us
    all_to_all x0 -> x4, waiting for transfers between devices: none -> 216 us  [the longest x1 211 us: turn_halves(): lax.all_to_all(jnp.stack(lax.axis_size('expert') * [array_here], 0), 'exp...]
    all_gather x1 -> x0, waiting for transfers between devices: 65.3 us -> none  [local(): lax.all_gather(recv_dy[None], 'expert', axis=0, tiled=True)]
    all_gather x1, waiting for transfers between devices: 33.9 us -> 0.01 us  [local(): lax.all_gather(recv_x[None], 'expert', axis=0, tiled=True)]
    all_to_all x3 -> x0, blocking collectives: 31.6 us -> none  [the longest x1 12.8 us: local(): lax.all_to_all(send_dy, 'dp', split_axis=0, concat_axis=0, tiled=True)]
    all_to_all x0 -> x4, starting transfers between devices: none -> 26.7 us  [the longest x1 10.7 us: turn_halves(): lax.all_to_all(jnp.stack(lax.axis_size('expert') * [array_here], 0), 'exp...]
    another operation x1 -> x3, local copies, waits for them, and re-layouts: 0.01 us -> 22.1 us  [the longest x1 18.1 us: full_rows(): gathered.reshape(n_groups, n_sources, capacity, part_width)]
    reshape x2 -> x1, local copies, waits for them, and re-layouts: 36.4 us -> 18.3 us  [full_rows(): gathered.reshape(n_groups, n_sources, capacity, part_width)]
    unnamed x4 -> x3, waiting for transfers between devices: 30.9 us -> 32.3 us
  transfers between devices with their start and end apart: 5 -> 8, of which waited for: 4 -> 4; matrix products, arithmetic and copies ran while one was open for 17% -> 16% of each run, Pallas kernels for 0% -> 0%
where the time goes in v1:
time: 729 us; the launch traced here: 719 us
  waiting for transfers between devices  251 us (34%)
  local copies, waits for them, and re-layouts  182 us (25%)
  blocking collectives  118 us (16%)
  starting transfers between devices  66.3 us (9%)
  matrix products  61.5 us (8%)
  other arithmetic  24.7 us (3%)
  between operations  14.6 us (2%)
    all_to_all x1, waiting for transfers between devices, turn_halves(): lax.all_to_all(jnp.stack(lax.axis_size('expert') * [array_here], 0), 'exp...  211 us
    psum x1, blocking collectives, local(): lax.psum(back_part.astype(jnp.bfloat16), 'expert').astype(jnp.float32)  118 us
    dot_general x15, matrix products, product(): jnp.einsum(pattern, operand_a, operand_b, preferred_element_type=jnp.floa...  52.5 us
    reshape x2, local copies, waits for them, and re-layouts, full_rows(): return ordered.reshape(n_sources * capacity, n_groups * part_width)  36.7 us
    all_to_all x1, starting transfers between devices, local(): lax.all_to_all(gate_dots.reshape(n_experts, capacity).astype(jnp.bfloat16...  34 us
    unnamed x3, waiting for transfers between devices  32.3 us
    convert_element_type x2, local copies, waits for them, and re-layouts, local(): term.reshape(1 * lax.axis_size('expert'), own_rows * part_width)  29.3 us
    transpose x2, local copies, waits for them, and re-layouts, full_rows(): gathered.reshape(n_groups, n_sources, capacity, part_width)  27.7 us
  transfers between devices with their start and end apart: 8, of which 4 were waited for; matrix products, arithmetic and copies ran while one was open for 16% of the time, Pallas kernels for 0%

profile of v1, /device:TPU:1, one launch (start us, length us, event | category | flops | bytes accessed | tf_op | source)
XLA Modules:
  0.0 719.1 jit_solution(5065830964357112226)
XLA Ops:
  11.8 6.4 all-to-all-start
  20.0 1.9 broadcast_in_dim.54
  21.9 1.9 reshape.231
  26.9 2.1 all_to_all.35
  29.5 3.0 reduce.16
  33.4 4.8 all-to-all-start.1
  38.3 1.8 copy.108
  40.1 2.1 all_to_all.36
  42.2 3.7 reduce.17
  47.7 4.8 all-to-all-start.3
  54.5 4.4 all-to-all-done.3
  58.9 4.0 stack.12
  62.9 10.7 %all-to-all-start.2 = ((bf16[32,1,8,15360]{3,2,1,0:T(8,128)(2,1)}), bf16[32,1,8,15360]{3,2,1,0:T(8,128)(2,1)}, u32[]{:S(2)}, u32[]{:S(2)}) async-start(bf16[32,1,8,15360]{3,2,1,0:T(8,128)(2,1)} %stack.12), calls=%async_computation.2 | async-start | bytes 15728640 | tf_op jit(solution)/shard_map/all_to_all | solution.py:10
  77.6 211.4 %all-to-all-done.2 = bf16[32,1,8,15360]{3,2,1,0:T(8,128)(2,1)} async-done(((bf16[32,1,8,15360]{3,2,1,0:T(8,128)(2,1)}), bf16[32,1,8,15360]{3,2,1,0:T(8,128)(2,1)}, u32[]{:S(2)}, u32[]{:S(2)}) %all-to-all-start.2) | async-done | bytes 7864352 | tf_op jit(solution)/shard_map/all_to_all | solution.py:10
  289.1 18.1 %reshape_reshape.3 = bf16[32,8,80,192]{3,2,1,0:T(8,128)(2,1)} reshape(bf16[32,1,8,15360]{3,2,1,0:T(8,128)(2,1)} %all-to-all-done.2) | data formatting | bytes 15728640 | tf_op jit(solution)/shard_map/reshape;reshape | solution.py:26
  307.1 13.8 %copy.106 = bf16[8,80,32,192]{3,2,1,0:T(8,128)(2,1)} copy(bf16[8,80,32,192]{3,1,0,2:T(8,128)(2,1)} %bitcast.106) | data formatting | bytes 15728640 | tf_op jit(solution)/shard_map/transpose | solution.py:26
  321.0 18.1 %reshape.232 = bf16[640,6144]{1,0:T(8,128)(2,1)} reshape(bf16[8,80,32,192]{3,2,1,0:T(8,128)(2,1)} %copy.106) | data formatting | bytes 15728640 | tf_op jit(solution)/shard_map/reshape | solution.py:27
  339.1 5.5 convolution_bitcast_fusion
  344.7 5.4 fusion.7
  350.1 18.3 %reshape.233 = bf16[32,8,80,192]{3,2,1,0:T(8,128)(2,1)} reshape(bf16[256,1,15360]{2,0,1:T(8,128)(2,1)} %all-gather.3.cloned.1.call-done) | data formatting | bytes 15728640 | tf_op jit(solution)/shard_map/reshape | solution.py:26
  368.3 13.8 %copy.111 = bf16[8,80,32,192]{3,2,1,0:T(8,128)(2,1)} copy(bf16[8,80,32,192]{3,1,0,2:T(8,128)(2,1)} %bitcast.107) | data formatting | bytes 15728640 | tf_op jit(solution)/shard_map/transpose | solution.py:26
  382.2 18.5 %reshape.234 = bf16[640,6144]{1,0:T(8,128)(2,1)} reshape(bf16[8,80,32,192]{3,2,1,0:T(8,128)(2,1)} %copy.111) | data formatting | bytes 15728640 | tf_op jit(solution)/shard_map/reshape | solution.py:27
  400.7 5.8 convolution_convert_fusion
  406.6 2.9 fusion.3
  409.5 2.9 fusion.5
  414.3 6.8 fusion.25
  421.1 8.8 %fusion.2 = bf16[32,640,192]{1,2,0:T(8,128)(2,1)} fusion(f32[640,32,192]{0,2,1:T(8,128)} %fusion.25, bf16[32,192,256]{2,1,0:T(8,128)(2,1)S(1)} %bitcast.108, bf16[640,256]{0,1:T(8,128)(2,1)S(1)} %get-tuple-element.44), kind=kOutput, calls=%fused_computation.7 | convolution fusion | flops 2021130240 | bytes 27066368 | tf_op jit(solution)/shard_map/nf,kdf->knd/dot_general | solution.py:15
  430.0 13.7 %copy.114 = bf16[32,640,192]{2,1,0:T(8,128)(2,1)} copy(bf16[32,640,192]{1,2,0:T(8,128)(2,1)} %fusion.2) | data formatting | bytes 15728640 | tf_op jit(solution)/shard_map/convert_element_type | solution.py:131
  443.7 15.6 %convert_element_type.158 = bf16[32,122880]{1,0:T(8,128)(2,1)} reshape(bf16[32,640,192]{2,1,0:T(8,128)(2,1)} %copy.114) | data formatting | bytes 15728640 | tf_op jit(solution)/shard_map/convert_element_type | solution.py:131
  464.3 118.5 %all-reduce.1 = (bf16[32,640]{1,0:T(8,128)(2,1)S(1)}, bf16[16,640]{1,0:T(8,128)(2,1)S(1)}, bf16[640]{0:T(1024)(128)(2,1)S(1)}) all-reduce(bf16[32,640]{1,0:T(8,128)(2,1)S(1)} %pad_maximum_fusion.1, bf16[16,640]{1,0:T(8,128)(2,1)S(1)} %fusion.18, bf16[640]{0:T(1024)(128)(2,1)S(1)} %get-tuple-element.41), channel_id=1, replica_groups=mesh['dp'=8,'expert'=32] {'expert'}, use_global_device_ids=true, to_apply=%region_5.6 | all-reduce | flops 31360 | bytes 125440 | tf_op jit(solution)/shard_map/psum | solution.py:118
  583.5 34.0 %all-to-all-start.5 = ((bf16[8,1,80]{2,1,0:T(2,128)(2,1)}), bf16[8,1,80]{2,1,0:T(2,128)(2,1)S(1)}, u32[]{:S(2)}, u32[]{:S(2)}) async-start(bf16[8,1,80]{2,1,0:T(2,128)(2,1)} %convert_element_type.182), calls=%async_computation.5 | async-start | bytes 8192 | tf_op jit(solution)/shard_map/all_to_all | solution.py:151
  619.8 1.9 fusion.19
  621.7 5.3 fusion.1
  626.9 5.7 fusion
  633.3 2.3 gather_fusion.1
  636.4 32.2 %all-reduce.4.cloned.1.call-done = bf16[32,122880]{1,0:T(8,128)(2,1)} async-done(((bf16[32,122880]{1,0:T(8,128)(2,1)}), bf16[32,122880]{1,0:T(8,128)(2,1)}) %all-reduce.4.cloned.1.call-update) | async-done | bytes 7864336
  668.7 4.4 fusion.22
  673.1 2.0 reshape.240
  675.1 2.1 copy.115
  679.5 2.1 convert_element_type.181
  681.6 3.0 reduce.18
  685.5 5.3 all-to-all-start.4
  694.1 3.0 all-to-all-done.4
  698.0 3.2 convert_reduce_fusion
  701.2 2.2 reshape.241
  703.4 3.3 gather_fusion
  706.7 2.1 gather.13
  708.8 2.4 select_reduce_fusion.1
  (91 shorter events, 38.2 us)
Async XLA Ops:
  7.2 399.4 %copy-start = (bf16[1,6144,256]{2,1,0:T(8,128)(2,1)S(1)}, bf16[1,6144,256]{2,1,0:T(8,128)(2,1)}, u32[]{:S(2)}) copy-start(bf16[1,6144,256]{2,1,0:T(8,128)(2,1)} %param.15) | copy-start | bytes 9437188
  11.8 21.6 %all-to-all-start = ((bf16[8,1,80]{2,1,0:T(2,128)(2,1)}), bf16[8,1,80]{2,1,0:T(2,128)(2,1)S(1)}, u32[]{:S(2)}, u32[]{:S(2)}) async-start(bf16[8,1,80]{2,1,0:T(2,128)(2,1)} %convert_element_type.180), calls=%async_computation | async-start | bytes 8192 | tf_op jit(solution)/shard_map/all_to_all | solution.py:73
  33.4 14.3 %all-to-all-start.1 = ((bf16[8,2,7680]{2,1,0:T(2,128)(2,1)}), bf16[8,2,7680]{2,1,0:T(2,128)(2,1)S(1)}, u32[]{:S(2)}, u32[]{:S(2)}) async-start(bf16[8,2,7680]{2,1,0:T(2,128)(2,1)} %reshape.288), calls=%async_computation.1 | async-start | bytes 491520 | tf_op jit(solution)/shard_map/all_to_all | solution.py:72
  47.7 11.2 %all-to-all-start.3 = ((bf16[8,2,7680]{2,1,0:T(2,128)(2,1)}), bf16[8,2,7680]{2,1,0:T(2,128)(2,1)}, u32[]{:S(2)}, u32[]{:S(2)}) async-start(bf16[8,2,7680]{2,1,0:T(2,128)(2,1)} %reshape.286), calls=%async_computation.3 | async-start | bytes 491520 | tf_op jit(solution)/shard_map/all_to_all | solution.py:71
  62.9 226.1 %all-to-all-start.2 = ((bf16[32,1,8,15360]{3,2,1,0:T(8,128)(2,1)}), bf16[32,1,8,15360]{3,2,1,0:T(8,128)(2,1)}, u32[]{:S(2)}, u32[]{:S(2)}) async-start(bf16[32,1,8,15360]{3,2,1,0:T(8,128)(2,1)} %stack.12), calls=%async_computation.2 | async-start | bytes 15728640 | tf_op jit(solution)/shard_map/all_to_all | solution.py:10
  73.6 276.4 %all-gather.3.cloned.1.call-start = ((), (), s32[]{:S(2)}) async-start(), calls=%async_computation.6 | async-start | bytes 8110080 | tf_op jit(solution)/shard_map/all_gather | solution.py:77
  77.3 591.4 %all-reduce.4.cloned.1.call-start = ((), (), s32[]{:S(2)}) async-start(), calls=%async_computation.7 | async-start | bytes 15728640
  321.0 18.2 %copy-start.8 = (bf16[1,16,6144]{2,1,0:T(8,128)(2,1)S(1)}, bf16[1,16,6144]{2,1,0:T(8,128)(2,1)}, u32[]{:S(2)}) copy-start(bf16[1,16,6144]{2,1,0:T(8,128)(2,1)} %param.21) | copy-start | bytes 589828
  339.1 5.5 copy-start.1
  400.7 5.8 copy-start.2
  406.5 2.9 copy-start.3
  409.4 3.0 copy-start.10
  409.4 3.3 copy-start.6
  409.4 3.3 copy-start.11
  414.3 6.8 copy-start.5
  414.3 6.8 copy-start.4
  459.2 1.0 copy-start.12
  582.7 49.9 %copy-start.7 = (bf16[32,640]{1,0:T(8,128)(2,1)}, bf16[32,640]{1,0:T(8,128)(2,1)S(1)}, u32[]{:S(2)}) copy-start(bf16[32,640]{1,0:T(8,128)(2,1)S(1)} %get-tuple-element.36) | copy-start | bytes 122884
  583.5 49.8 %all-to-all-start.5 = ((bf16[8,1,80]{2,1,0:T(2,128)(2,1)}), bf16[8,1,80]{2,1,0:T(2,128)(2,1)S(1)}, u32[]{:S(2)}, u32[]{:S(2)}) async-start(bf16[8,1,80]{2,1,0:T(2,128)(2,1)} %convert_element_type.182), calls=%async_computation.5 | async-start | bytes 8192 | tf_op jit(solution)/shard_map/all_to_all | solution.py:151
  685.5 11.6 %all-to-all-start.4 = ((bf16[8,2,7680]{2,1,0:T(2,128)(2,1)}), bf16[8,2,7680]{2,1,0:T(2,128)(2,1)S(1)}, u32[]{:S(2)}, u32[]{:S(2)}) async-start(bf16[8,2,7680]{2,1,0:T(2,128)(2,1)} %reshape.290), calls=%async_computation.4 | async-start | bytes 491520 | tf_op jit(solution)/shard_map/all_to_all | solution.py:144
  698.0 10.8 %copy-start.9 = (pred[256,2]{1,0:T(8,128)(4,1)S(1)}, pred[256,2]{1,0:T(8,128)(4,1)}, u32[]{:S(2)}) copy-start(pred[256,2]{1,0:T(8,128)(4,1)} %get-tuple-element.40) | copy-start | bytes 1540
Sparse Core Ops, SparseCore 0:
  77.6 206.5 all-gather.2
  459.4 209.2 all-reduce.3
